TPU v7x, 256 devices: a whole 4x4x8 slice. The times are simulated.
256 devices in a mesh: region: 16 (over x, y_lo, core), patch: 16 (over z, y_hi).
Axes of the slice: x: 4, y: 4 (y_hi: 2, y_lo: 2; y = y_hi * 2 + y_lo), z: 8, core: 2. Of those that a mesh axis runs over, the one named last changes fastest.
Arguments:
- nodes: bfloat16 [65536, 512], P(('region', 'patch')), may hold values from -6 to 6
- edges: bfloat16 [524288, 512], P(('region', 'patch')), may hold values from -6 to 6
- senders: int32 [524288], P(('region', 'patch')), may hold values from 0 to 799, as said below
- receivers: int32 [524288], P(('region', 'patch')), may hold values from 0 to 767, as said below
- valid_counts: int32 [256], P(('region', 'patch')), may hold values from 512 to 2048, as said below
- hub_owner: int32 [2, 16], P(None, 'region'), may hold values from 0 to 15
- edge_in: bfloat16 [2, 3, 512, 512], replicated, may hold values from -0.15625 to 0.15625
- edge_bias: float32 [2, 512], replicated, may hold values from -3 to 3
- edge_out: bfloat16 [2, 512, 512], replicated, may hold values from -0.25 to 0.25
- edge_gain: float32 [2, 512], replicated, may hold values from 0.25 to 1.75
- edge_shift: float32 [2, 512], replicated, may hold values from -2 to 2
- node_in: bfloat16 [2, 2, 512, 512], replicated, may hold values from -0.1875 to 0.1875
- node_bias: float32 [2, 512], replicated, may hold values from -3 to 3
- node_out: bfloat16 [2, 512, 512], replicated, may hold values from -0.25 to 0.25
- node_gain: float32 [2, 512], replicated, may hold values from 0.25 to 1.75
- node_shift: float32 [2, 512], replicated, may hold values from -2 to 2
Outputs:
- nodes_out: bfloat16 [65536, 512], P(('region', 'patch'))
- edges_out: bfloat16 [524288, 512], P(('region', 'patch'))
Inputs may be any that keep to these rules, and one draw needn't show every extreme that they name: `senders`: codes below 256 name a row of the previous patch, below 512 of the own patch, below 768 of the next patch, the rest a hub row. `receivers`: codes below 256 name a row of the previous patch, below 512 of the own patch, the rest of the next patch. `valid_counts`: live slots are the first ones of a patch; some patch has all 2048 slots live.
All inputs are finite; a program needn't handle non-finite values.
Results may differ from a plain program's by a relative error of at most 0.012.
Values may be sent and summed in bfloat16 or wider, within the bound.
A program may use at most 64 MiB of HBM per device.

v0:
```python
import jax
import jax.numpy as jnp
from jax import lax
from jax.sharding import Mesh
from jax.sharding import PartitionSpec as P

HUB = 32
LAYERS = 2
PATCH = ("patch_0", "patch_1")
REGION_PATCH = ("region", "patch_0", "patch_1")


epsilon = 1e-05


def extended(cells, sides, width):
    for axis, dim in sides:
        count = lax.axis_size(axis)
        head = lax.slice_in_dim(cells, 0, width, axis=dim)
        tail = lax.slice_in_dim(cells, cells.shape[dim] - width, cells.shape[dim], axis=dim)
        cells = jnp.concatenate(
            [
                lax.ppermute(tail, axis, [(i, (i + 1) % count) for i in range(count)]),
                cells,
                lax.ppermute(head, axis, [((i + 1) % count, i) for i in range(count)]),
            ],
            axis=dim,
        )
    return cells


def broadcast_by_axis(array, axes, root):
    array = jnp.where(lax.axis_index(axes) == root, array, jnp.zeros_like(array))
    for axis in axes:
        array = lax.psum(array, axis)
    return array


def from_behind(block, axis, distance):
    devices = range(lax.axis_size(axis))
    route = [((i - distance) % len(devices), i) for i in devices]
    return lax.ppermute(block, axis, route)


def activate(value):
    return value / (1.0 + jnp.exp(-value))


def layer_norm(value, gain, shift):
    center = value - jnp.mean(value, axis=-1, keepdims=True)
    spread = jnp.mean(center * center, axis=-1, keepdims=True)
    return center * lax.rsqrt(spread + epsilon) * gain + shift


def update_edges(
    edge_block,
    send_codes,
    recv_codes,
    send_table,
    recv_table,
    first_weight,
    first_bias,
    second_weight,
    gain,
    shift,
):
    pre_edge = jnp.dot(edge_block, first_weight, preferred_element_type=jnp.float32)
    pre_edge = pre_edge + jnp.take(send_table, send_codes, axis=0).astype(jnp.float32)
    pre_edge = pre_edge + jnp.take(recv_table, recv_codes, axis=0).astype(jnp.float32)
    pre_edge = pre_edge + first_bias
    activated = activate(pre_edge).astype(jnp.bfloat16)
    mixed = jnp.dot(activated, second_weight, preferred_element_type=jnp.float32)
    return edge_block.astype(jnp.float32) + layer_norm(mixed, gain, shift)


def local(
    nodes,
    edges,
    senders,
    receivers,
    valid_counts,
    hub_owner,
    edge_in,
    edge_bias,
    edge_out,
    edge_gain,
    edge_shift,
    node_in,
    node_bias,
    node_out,
    node_gain,
    node_shift,
):
    node_rows = nodes.shape[0]
    features = nodes.shape[1]
    edge_rows = edges.shape[0]
    valid_rows = valid_counts[0]
    positions = lax.broadcasted_iota(jnp.int32, (edge_rows,), 0)
    is_valid = positions < valid_rows
    for layer_index in range(LAYERS):
        holder = hub_owner[layer_index, 0]
        both_weights = jnp.concatenate([edge_in[layer_index, 1], edge_in[layer_index, 2]], axis=1)
        own_proj = jnp.dot(nodes, both_weights, preferred_element_type=jnp.float32).astype(
            jnp.bfloat16
        )
        proj_table = extended(own_proj, ((PATCH, 0),), node_rows)
        hub_send = broadcast_by_axis(own_proj[:HUB, :features], PATCH, holder)
        send_table = jnp.concatenate([proj_table[:, :features], hub_send], axis=0)
        recv_table = proj_table[:, features:]
        first_weight = edge_in[layer_index, 0]
        first_bias = edge_bias[layer_index]
        second_weight = edge_out[layer_index]
        gain = edge_gain[layer_index]
        shift = edge_shift[layer_index]
        updated = update_edges(
            edges,
            senders,
            receivers,
            send_table,
            recv_table,
            first_weight,
            first_bias,
            second_weight,
            gain,
            shift,
        )
        new_edges = jnp.where(is_valid[:, None], updated, 0.0).astype(jnp.bfloat16)
        edges = new_edges
        partial_value = jax.ops.segment_sum(
            edges.astype(jnp.float32), receivers, num_segments=3 * node_rows
        )
        from_next = from_behind(partial_value[:node_rows].astype(jnp.bfloat16), PATCH, -1).astype(
            jnp.float32
        )
        from_prev = from_behind(
            partial_value[2 * node_rows :].astype(jnp.bfloat16), PATCH, 1
        ).astype(jnp.float32)
        aggregate = (from_prev + partial_value[node_rows : 2 * node_rows] + from_next).astype(
            jnp.bfloat16
        )
        pre_node = jnp.dot(nodes, node_in[layer_index, 0], preferred_element_type=jnp.float32)
        pre_node = pre_node + jnp.dot(
            aggregate, node_in[layer_index, 1], preferred_element_type=jnp.float32
        )
        pre_node = pre_node + node_bias[layer_index]
        node_act = activate(pre_node).astype(jnp.bfloat16)
        node_mixed = jnp.dot(node_act, node_out[layer_index], preferred_element_type=jnp.float32)
        nodes = (
            nodes.astype(jnp.float32)
            + layer_norm(node_mixed, node_gain[layer_index], node_shift[layer_index])
        ).astype(jnp.bfloat16)
    return (nodes, edges)


def solution(mesh):
    torus = Mesh(mesh.devices.reshape(mesh.shape["region"], 8, 2), ("region", "patch_0", "patch_1"))
    return jax.shard_map(
        local,
        mesh=torus,
        in_specs=(
            P(REGION_PATCH, None),
            P(REGION_PATCH, None),
            P(REGION_PATCH),
            P(REGION_PATCH),
            P(REGION_PATCH),
            P(None, "region"),
            P(),
            P(),
            P(),
            P(),
            P(),
            P(),
            P(),
            P(),
            P(),
            P(),
        ),
        out_specs=(P(REGION_PATCH, None), P(REGION_PATCH, None)),
        check_vma=False,
    )
```

profile of v0, /device:TPU:4, one launch (start us, length us, event | category | flops | bytes accessed | tf_op | source)
XLA Modules:
  0.0 243.9 jit_solution(373921147333139942)
XLA Ops:
  3.9 3.3 %collective-permute-start = (bf16[256,1024]{1,0:T(8,128)(2,1)S(1)}, bf16[256,1024]{1,0:T(8,128)(2,1)S(1)}, u32[]{:S(2)}, u32[]{:S(2)}) collective-permute-start(bf16[256,1024]{1,0:T(8,128)(2,1)S(1)} %fusion.6), channel_id=1, source_target_pairs={{0,1},{1,2},{2,3},{3,4},{4,5},{5,6},{6,7},{7,8},{8,9},{9,10},{10,1... | collective-permute-start | bytes 1572872 | tf_op jit(solution)/shard_map/ppermute | solution.py:23
  7.1 5.4 %collective-permute-start.1 = (bf16[256,1024]{1,0:T(8,128)(2,1)S(1)}, bf16[256,1024]{1,0:T(8,128)(2,1)}, u32[]{:S(2)}, u32[]{:S(2)}) collective-permute-start(bf16[256,1024]{1,0:T(8,128)(2,1)S(1)} %fusion.6), channel_id=1, source_target_pairs={{1,0},{2,1},{3,2},{4,3},{5,4},{6,5},{7,6},{8,7},{9,8},{10,9},{11,1... | collective-permute-start | bytes 1572872 | tf_op jit(solution)/shard_map/ppermute | solution.py:25
  13.8 34.5 %psum.28 = bf16[32,512]{1,0:T(8,128)(2,1)S(1)} all-reduce(bf16[32,512]{1,0:T(8,128)(2,1)S(1)} %slice_select_fusion.1), channel_id=1, replica_groups=mesh['region'=16,'patch_0'=8,'patch_1'=2] {'patch_0'}, use_global_device_ids=true, to_apply=%region_0.1 | all-reduce | flops 16384 | bytes 65536 | tf_op jit(solution)/shard_map/psum | solution.py:35
  48.4 8.4 %psum.29 = bf16[32,512]{1,0:T(8,128)(2,1)S(1)} all-reduce(bf16[32,512]{1,0:T(8,128)(2,1)S(1)} %psum.28), channel_id=1, replica_groups=mesh['region'=16,'patch_0'=8,'patch_1'=2] {'patch_1'}, use_global_device_ids=true, to_apply=%region_1.2 | all-reduce | flops 16384 | bytes 65536 | tf_op jit(solution)/shard_map/psum | solution.py:35
  61.4 9.2 %gather_fusion = bf16[2048,512]{1,0:T(8,128)(2,1)} fusion(bf16[800,512]{1,0:T(8,128)(2,1)S(1)} %pad_maximum_fusion.2, s32[2048]{0:T(1024)S(1)} %fusion.71), kind=kCustom, calls=%fused_computation.clone | custom fusion | bytes 4202496 | tf_op jit(solution)/shard_map/jit(_take)/gather | solution.py:68
  70.6 9.2 %gather_fusion.1 = bf16[2048,512]{1,0:T(8,128)(2,1)} fusion(bf16[768,512]{1,0:T(8,128)(2,1)S(1)} %get-tuple-element.15, s32[2048]{0:T(1024)S(1)} %fusion.72), kind=kCustom, calls=%fused_computation.1.clone | custom fusion | bytes 4202496 | tf_op jit(solution)/shard_map/jit(_take)/gather | solution.py:69
  79.8 6.6 %fusion.92 = (f32[2048]{0:T(1024)S(1)}, f32[2048,512]{0,1:T(8,128)}) fusion(bf16[2,512,512]{2,1,0:T(8,128)(2,1)} %param.28, bf16[2048,512]{1,0:T(8,128)(2,1)} %gather_fusion.1, bf16[2048,512]{1,0:T(8,128)(2,1)S(1)} %copy-done.4, f32[512]{0:T(512)S(1)} %bitcast.99, pred[2048]{0:T(1024)(128)(4,1)S(1)} %get-tuple-element.42, ...), kind=kOutput, calls=%fused_computation.119 | convolution fusion | flops 2160064512 | bytes 11548672 | tf_op jit(solution)/shard_map/dot_general | solution.py:72
  86.4 2.8 %multiply_reduce_fusion.1 = f32[2048]{0:T(1024)S(1)} fusion(f32[2048,512]{0,1:T(8,128)} %get-tuple-element.35, f32[2048]{0:T(1024)S(1)} %broadcast_multiply_fusion.1), kind=kLoop, calls=%fused_computation.10 | loop fusion | flops 3143680 | bytes 4210688 | tf_op jit(solution)/shard_map/reduce_sum | solution.py:51
  89.9 2.8 %select_convert_fusion.1 = bf16[2048,512]{0,1:T(8,128)(2,1)S(1)} fusion(bf16[2048,512]{0,1:T(8,128)(2,1)} %copy.20, f32[2048,512]{0,1:T(8,128)S(1)} %copy-done.3, f32[512]{0:T(512)S(1)} %bitcast.93, f32[512]{0:T(512)S(1)} %bitcast.94, f32[2048]{0:T(1024)S(1)} %add_rsqrt_fusion.1, f32[2048]{0:T(1024)S(1)} %broadcast_multiply_fusion.1, ...), kind=kLoop, calls=%fused_computation.9 | loop fusion | flops 8388608 | bytes 8411136 | tf_op jit(solution)/shard_map/convert_element_type | solution.py:127
  92.6 3.1 %copy.21 = f32[2048,512]{1,0:T(8,128)} copy(bf16[2048,512]{0,1:T(8,128)(2,1)S(1)} %select_convert_fusion.1) | data formatting | bytes 6291456 | tf_op jit(solution)/shard_map/convert_element_type | solution.py:130
  95.7 14.4 %scatter_custom_fusion = f32[768,512]{1,0:T(8,128)} fusion(s32[2048]{0:T(1024)S(1)} %copy-done.9, f32[2048,512]{1,0:T(8,128)} %copy.21, f32[]{:T(128)} %constant.25.clone.1), kind=kCustom, calls=%fused_computation.37 | custom fusion | flops 1048576 | bytes 1573376 | tf_op jit(solution)/shard_map/scatter-add | solution.py:129
  111.8 3.5 %collective-permute-start.2 = (bf16[256,512]{1,0:T(8,128)(2,1)S(1)}, bf16[256,512]{1,0:T(8,128)(2,1)S(1)}, u32[]{:S(2)}, u32[]{:S(2)}) collective-permute-start(bf16[256,512]{1,0:T(8,128)(2,1)S(1)} %get-tuple-element.18), channel_id=1, source_target_pairs={{15,0},{0,1},{1,2},{2,3},{3,4},{4,5},{5,6},{6,7},{7,8},{8,9},{9,10... | collective-permute-start | bytes 786440 | tf_op jit(solution)/shard_map/ppermute | solution.py:42
  117.9 4.2 %collective-permute-done.2 = bf16[256,512]{1,0:T(8,128)(2,1)S(1)} collective-permute-done((bf16[256,512]{1,0:T(8,128)(2,1)S(1)}, bf16[256,512]{1,0:T(8,128)(2,1)S(1)}, u32[]{:S(2)}, u32[]{:S(2)}) %collective-permute-start.2) | collective-permute-done | bytes 262176 | tf_op jit(solution)/shard_map/ppermute | solution.py:42
  131.0 4.2 %collective-permute-start.5 = (bf16[256,1024]{1,0:T(8,128)(2,1)S(1)}, bf16[256,1024]{1,0:T(8,128)(2,1)S(1)}, u32[]{:S(2)}, u32[]{:S(2)}) collective-permute-start(bf16[256,1024]{1,0:T(8,128)(2,1)S(1)} %convolution_convert_fusion.1), channel_id=1, source_target_pairs={{1,0},{2,1},{3,2},{4,3},{5,4},{6,5},{7,6},{8,7},{9,8},{10,9},{11,1... | collective-permute-start | bytes 1572872 | tf_op jit(solution)/shard_map/ppermute | solution.py:25
  135.9 30.6 %psum.30 = bf16[32,512]{1,0:T(8,128)(2,1)S(1)} all-reduce(bf16[32,512]{1,0:T(8,128)(2,1)S(1)} %slice_select_fusion), channel_id=1, replica_groups=mesh['region'=16,'patch_0'=8,'patch_1'=2] {'patch_0'}, use_global_device_ids=true, to_apply=%region_7.10 | all-reduce | flops 16384 | bytes 65536 | tf_op jit(solution)/shard_map/psum | solution.py:35
  166.5 8.4 %psum.31 = bf16[32,512]{1,0:T(8,128)(2,1)S(1)} all-reduce(bf16[32,512]{1,0:T(8,128)(2,1)S(1)} %psum.30), channel_id=1, replica_groups=mesh['region'=16,'patch_0'=8,'patch_1'=2] {'patch_1'}, use_global_device_ids=true, to_apply=%region_8.11 | all-reduce | flops 16384 | bytes 65536 | tf_op jit(solution)/shard_map/psum | solution.py:35
  175.3 9.2 %gather_fusion.2 = bf16[2048,512]{1,0:T(8,128)(2,1)} fusion(bf16[800,512]{1,0:T(8,128)(2,1)S(1)} %pad_maximum_fusion.3, s32[2048]{0:T(1024)S(1)} %fusion.71), kind=kCustom, calls=%fused_computation.2.clone | custom fusion | bytes 4202496 | tf_op jit(solution)/shard_map/jit(_take)/gather | solution.py:68
  184.5 9.2 %gather_fusion.3 = bf16[2048,512]{1,0:T(8,128)(2,1)} fusion(bf16[768,512]{1,0:T(8,128)(2,1)S(1)} %get-tuple-element.13, s32[2048]{0:T(1024)S(1)} %fusion.72), kind=kCustom, calls=%fused_computation.3.clone | custom fusion | bytes 4202496 | tf_op jit(solution)/shard_map/jit(_take)/gather | solution.py:69
  193.7 7.9 %fusion.100 = (f32[2048]{0:T(1024)S(1)}, f32[2048,512]{0,1:T(8,128)}) fusion(bf16[2,512,512]{2,1,0:T(8,128)(2,1)} %param.28, bf16[2048,512]{1,0:T(8,128)(2,1)} %gather_fusion.3, bf16[2048,512]{1,0:T(8,128)(2,1)} %gather_fusion.2, f32[512]{0:T(512)S(1)} %bitcast.97, pred[2048]{0:T(1024)(128)(4,1)S(1)} %get-tuple-element.42, ...), kind=kOutput, calls=%fused_computation.121 | convolution fusion | flops 2160064512 | bytes 11548672 | tf_op jit(solution)/shard_map/dot_general | solution.py:72
  201.6 2.8 %multiply_reduce_fusion = f32[2048]{0:T(1024)S(1)} fusion(f32[2048,512]{0,1:T(8,128)} %get-tuple-element.39, f32[2048]{0:T(1024)S(1)} %broadcast_multiply_fusion), kind=kLoop, calls=%fused_computation.7 | loop fusion | flops 3143680 | bytes 4210688 | tf_op jit(solution)/shard_map/reduce_sum | solution.py:51
  204.5 3.3 %select_convert_fusion = bf16[2048,512]{0,1:T(8,128)(2,1)S(1)} fusion(f32[2048,512]{0,1:T(8,128)} %get-tuple-element.39, f32[512]{0:T(512)S(1)} %bitcast.89, f32[512]{0:T(512)S(1)} %bitcast.90, f32[2048]{0:T(1024)S(1)} %add_rsqrt_fusion, f32[2048]{0:T(1024)S(1)} %broadcast_multiply_fusion, pred[2048]{0:T(1024)(128)(4,1)S(1)} %iota_compare_fusion, ...), kind=kLoop, calls=%fused_computation.6 | loop fusion | flops 8388608 | bytes 8411136 | tf_op jit(solution)/shard_map/convert_element_type | solution.py:127
  207.8 3.0 %copy.22 = f32[2048,512]{1,0:T(8,128)} copy(bf16[2048,512]{0,1:T(8,128)(2,1)S(1)} %select_convert_fusion) | data formatting | bytes 6291456 | tf_op jit(solution)/shard_map/convert_element_type | solution.py:130
  210.8 14.5 %scatter_custom_fusion.1 = f32[768,512]{1,0:T(8,128)} fusion(s32[2048]{0:T(1024)S(1)} %copy-done.9, f32[2048,512]{1,0:T(8,128)} %copy.22, f32[]{:T(128)} %constant.25.clone.1), kind=kCustom, calls=%fused_computation.35 | custom fusion | flops 1048576 | bytes 1573376 | tf_op jit(solution)/shard_map/scatter-add | solution.py:129
  227.5 3.5 %collective-permute-start.6 = (bf16[256,512]{1,0:T(8,128)(2,1)}, bf16[256,512]{1,0:T(8,128)(2,1)S(1)}, u32[]{:S(2)}, u32[]{:S(2)}) collective-permute-start(bf16[256,512]{1,0:T(8,128)(2,1)} %get-tuple-element.16), channel_id=1, source_target_pairs={{15,0},{0,1},{1,2},{2,3},{3,4},{4,5},{5,6},{6,7},{7,8},{8,9},{9,10... | collective-permute-start | bytes 786440 | tf_op jit(solution)/shard_map/ppermute | solution.py:42
  (92 shorter events, 36.9 us)
Async XLA Ops:
  0.6 2.8 %copy-start.6 = (bf16[256,512]{1,0:T(8,128)(2,1)S(1)}, bf16[256,512]{1,0:T(8,128)(2,1)}, u32[]{:S(2)}) copy-start(bf16[256,512]{1,0:T(8,128)(2,1)} %param.20) | copy-start | bytes 786436
  3.4 9.2 %copy-start.16 = (s32[2,1]{0,1:T(1,128)S(1)}, s32[2,1]{0,1:T(1,128)}, u32[]{:S(2)}) copy-start(s32[2,1]{0,1:T(1,128)} %param.25) | copy-start | bytes 28
  3.4 53.4 %copy-start.8 = (s32[2048]{0:T(1024)S(1)}, s32[2048]{0:T(1024)}, u32[]{:S(2)}) copy-start(s32[2048]{0:T(1024)} %param.22) | copy-start | bytes 24580
  3.4 53.4 %copy-start.10 = (f32[2,512]{1,0:T(2,128)S(1)}, f32[2,512]{1,0:T(2,128)}, u32[]{:S(2)}) copy-start(f32[2,512]{1,0:T(2,128)} %param.27) | copy-start | bytes 12292
  3.4 53.5 %copy-start.11 = (f32[2,512]{1,0:T(2,128)S(1)}, f32[2,512]{1,0:T(2,128)}, u32[]{:S(2)}) copy-start(f32[2,512]{1,0:T(2,128)} %param.30) | copy-start | bytes 12292
  3.4 53.5 %copy-start.12 = (f32[2,512]{1,0:T(2,128)S(1)}, f32[2,512]{1,0:T(2,128)}, u32[]{:S(2)}) copy-start(f32[2,512]{1,0:T(2,128)} %param.29) | copy-start | bytes 12292
  3.4 54.1 %copy-start.5 = (bf16[2048,512]{1,0:T(8,128)(2,1)S(1)}, bf16[2048,512]{1,0:T(8,128)(2,1)}, u32[]{:S(2)}) copy-start(bf16[2048,512]{1,0:T(8,128)(2,1)} %param.21) | copy-start | bytes 6291460
  3.9 56.2 %collective-permute-start = (bf16[256,1024]{1,0:T(8,128)(2,1)S(1)}, bf16[256,1024]{1,0:T(8,128)(2,1)S(1)}, u32[]{:S(2)}, u32[]{:S(2)}) collective-permute-start(bf16[256,1024]{1,0:T(8,128)(2,1)S(1)} %fusion.6), channel_id=1, source_target_pairs={{0,1},{1,2},{2,3},{3,4},{4,5},{5,6},{6,7},{7,8},{8,9},{9,10},{10,1... | collective-permute-start | bytes 1572872 | tf_op jit(solution)/shard_map/ppermute | solution.py:23
  7.1 52.9 %collective-permute-start.1 = (bf16[256,1024]{1,0:T(8,128)(2,1)S(1)}, bf16[256,1024]{1,0:T(8,128)(2,1)}, u32[]{:S(2)}, u32[]{:S(2)}) collective-permute-start(bf16[256,1024]{1,0:T(8,128)(2,1)S(1)} %fusion.6), channel_id=1, source_target_pairs={{1,0},{2,1},{3,2},{4,3},{5,4},{6,5},{7,6},{8,7},{9,8},{10,9},{11,1... | collective-permute-start | bytes 1572872 | tf_op jit(solution)/shard_map/ppermute | solution.py:25
  57.6 2.4 %copy-start.9 = (s32[2048]{0:T(1024)S(1)}, s32[2048]{0:T(1024)}, u32[]{:S(2)}) copy-start(s32[2048]{0:T(1024)} %param.23) | copy-start | bytes 24580
  70.6 9.2 %copy-start.4 = (bf16[2048,512]{1,0:T(8,128)(2,1)S(1)}, bf16[2048,512]{1,0:T(8,128)(2,1)}, u32[]{:S(2)}) copy-start(bf16[2048,512]{1,0:T(8,128)(2,1)} %gather_fusion) | copy-start | bytes 6291460
  86.4 3.4 %copy-start.3 = (f32[2048,512]{0,1:T(8,128)S(1)}, f32[2048,512]{0,1:T(8,128)}, u32[]{:S(2)}) copy-start(f32[2048,512]{0,1:T(8,128)} %get-tuple-element.35) | copy-start | bytes 12582916
  92.6 3.1 %copy-start = (bf16[2048,512]{0,1:T(8,128)(2,1)}, bf16[2048,512]{0,1:T(8,128)(2,1)S(1)}, u32[]{:S(2)}) copy-start(bf16[2048,512]{0,1:T(8,128)(2,1)S(1)} %select_convert_fusion.1) | copy-start | bytes 6291460
  110.1 7.4 %copy-start.15 = (f32[2,512]{1,0:T(2,128)S(1)}, f32[2,512]{1,0:T(2,128)}, u32[]{:S(2)}) copy-start(f32[2,512]{1,0:T(2,128)} %param.35) | copy-start | bytes 12292
  110.1 7.4 %copy-start.7 = (bf16[2,2,512,512]{3,2,1,0:T(8,128)(2,1)S(1)}, bf16[2,2,512,512]{3,2,1,0:T(8,128)(2,1)}, u32[]{:S(2)}) copy-start(bf16[2,2,512,512]{3,2,1,0:T(8,128)(2,1)} %param.31) | copy-start | bytes 6291460
  111.8 10.2 %collective-permute-start.2 = (bf16[256,512]{1,0:T(8,128)(2,1)S(1)}, bf16[256,512]{1,0:T(8,128)(2,1)S(1)}, u32[]{:S(2)}, u32[]{:S(2)}) collective-permute-start(bf16[256,512]{1,0:T(8,128)(2,1)S(1)} %get-tuple-element.18), channel_id=1, source_target_pairs={{15,0},{0,1},{1,2},{2,3},{3,4},{4,5},{5,6},{6,7},{7,8},{8,9},{9,10... | collective-permute-start | bytes 786440 | tf_op jit(solution)/shard_map/ppermute | solution.py:42
  115.4 9.3 %collective-permute-start.3 = (bf16[256,512]{1,0:T(8,128)(2,1)S(1)}, bf16[256,512]{1,0:T(8,128)(2,1)S(1)}, u32[]{:S(2)}, u32[]{:S(2)}) collective-permute-start(bf16[256,512]{1,0:T(8,128)(2,1)S(1)} %get-tuple-element.19), channel_id=1, source_target_pairs={{1,0},{2,1},{3,2},{4,3},{5,4},{6,5},{7,6},{8,7},{9,8},{10,9},{11,1... | collective-permute-start | bytes 786440 | tf_op jit(solution)/shard_map/ppermute | solution.py:42
  122.1 2.6 %copy-start.17 = (bf16[256,512]{1,0:T(8,128)(2,1)}, bf16[256,512]{1,0:T(8,128)(2,1)S(1)}, u32[]{:S(2)}) copy-start(bf16[256,512]{1,0:T(8,128)(2,1)S(1)} %collective-permute-done.2) | copy-start | bytes 786436
  129.5 45.4 %collective-permute-start.4 = (bf16[256,1024]{1,0:T(8,128)(2,1)S(1)}, bf16[256,1024]{1,0:T(8,128)(2,1)S(1)}, u32[]{:S(2)}, u32[]{:S(2)}) collective-permute-start(bf16[256,1024]{1,0:T(8,128)(2,1)S(1)} %convolution_convert_fusion.1), channel_id=1, source_target_pairs={{0,1},{1,2},{2,3},{3,4},{4,5},{5,6},{6,7},{7,8},{8,9},{9,10},{10,1... | collective-permute-start | bytes 1572872 | tf_op jit(solution)/shard_map/ppermute | solution.py:23
  131.0 43.9 %collective-permute-start.5 = (bf16[256,1024]{1,0:T(8,128)(2,1)S(1)}, bf16[256,1024]{1,0:T(8,128)(2,1)S(1)}, u32[]{:S(2)}, u32[]{:S(2)}) collective-permute-start(bf16[256,1024]{1,0:T(8,128)(2,1)S(1)} %convolution_convert_fusion.1), channel_id=1, source_target_pairs={{1,0},{2,1},{3,2},{4,3},{5,4},{6,5},{7,6},{8,7},{9,8},{10,9},{11,1... | collective-permute-start | bytes 1572872 | tf_op jit(solution)/shard_map/ppermute | solution.py:25
  184.5 9.2 %copy-start.1 = (bf16[2048,512]{0,1:T(8,128)(2,1)S(1)}, bf16[2048,512]{0,1:T(8,128)(2,1)}, u32[]{:S(2)}) copy-start(bf16[2048,512]{0,1:T(8,128)(2,1)} %copy-done) | copy-start | bytes 6291460
  201.6 2.9 %copy-start.2 = (bf16[2048,512]{0,1:T(8,128)(2,1)S(1)}, bf16[2048,512]{0,1:T(8,128)(2,1)}, u32[]{:S(2)}) copy-start(bf16[2048,512]{0,1:T(8,128)(2,1)} %copy-done) | copy-start | bytes 6291460
  227.5 10.5 %collective-permute-start.6 = (bf16[256,512]{1,0:T(8,128)(2,1)}, bf16[256,512]{1,0:T(8,128)(2,1)S(1)}, u32[]{:S(2)}, u32[]{:S(2)}) collective-permute-start(bf16[256,512]{1,0:T(8,128)(2,1)} %get-tuple-element.16), channel_id=1, source_target_pairs={{15,0},{0,1},{1,2},{2,3},{3,4},{4,5},{5,6},{6,7},{7,8},{8,9},{9,10... | collective-permute-start | bytes 786440 | tf_op jit(solution)/shard_map/ppermute | solution.py:42
  231.0 9.6 %collective-permute-start.7 = (bf16[256,512]{1,0:T(8,128)(2,1)S(1)}, bf16[256,512]{1,0:T(8,128)(2,1)}, u32[]{:S(2)}, u32[]{:S(2)}) collective-permute-start(bf16[256,512]{1,0:T(8,128)(2,1)S(1)} %get-tuple-element.17), channel_id=1, source_target_pairs={{1,0},{2,1},{3,2},{4,3},{5,4},{6,5},{7,6},{8,7},{9,8},{10,9},{11,1... | collective-permute-start | bytes 786440 | tf_op jit(solution)/shard_map/ppermute | solution.py:42
  (3 other events, 5.5 us)
where the time goes:
time: 244 us
  blocking collectives  82 us (34%)
  local copies, waits for them, and re-layouts  53.6 us (22%)
  other arithmetic  46.7 us (19%)
  starting transfers between devices  25.7 us (11%)
  matrix products  22.4 us (9%)
  waiting for transfers between devices  10.5 us (4%)
  between operations  3.04 us (1%)
    psum x4, blocking collectives, broadcast_by_axis(): array = lax.psum(array, axis)  82 us
    scatter-add x2, other arithmetic, local(): jax.ops.segment_sum(edges.astype(jnp.float32), receivers, num_segments=3...  28.9 us
    gather x2, local copies, waits for them, and re-layouts, update_edges(): jnp.take(recv_table, recv_codes, axis=0).astype(jnp.float32)  18.4 us
    gather x2, local copies, waits for them, and re-layouts, update_edges(): jnp.take(send_table, send_codes, axis=0).astype(jnp.float32)  18.4 us
    dot_general x2, matrix products, update_edges(): jnp.dot(activated, second_weight, preferred_element_type=jnp.float32)  14.5 us
    ppermute x4, starting transfers between devices, from_behind(): return lax.ppermute(block, axis, route)  11.4 us
    ppermute x4, waiting for transfers between devices, from_behind(): return lax.ppermute(block, axis, route)  10.5 us
    ppermute x2, starting transfers between devices, extended(): lax.ppermute(head, axis, [((i + 1) % count, i) for i in range(count)])  9.59 us
  transfers between devices with their start and end apart: 8, of which 4 were waited for; matrix products, arithmetic and copies ran while one was open for 3% of the time, Pallas kernels for 0%

commit v1 on v0

v1 whole, which is shorter than its diff:
```python
import functools

import jax
import jax.numpy as jnp
from jax import lax
from jax.experimental import pallas as pl
from jax.experimental.pallas import tpu as pltpu
from jax.sharding import PartitionSpec as P

HUB = 32
LAYERS = 2
GROUPS = ("region", "patch")
N_PATCH = 16
MESH = pl.DeviceIdType.MESH
EPS = 1e-05
TILE = 256
CHUNKS = 8
PIECES = 4
HUB_STAGES = ((1, 2, 3), (4, 8, 12))


def flipped(index, mask):
    for bit in (1, 2, 4, 8):
        if mask & bit:
            index = index + bit - 2 * bit * ((index // bit) % 2)
    return index


def silu(value):
    half = 0.5 * value
    return half + half * jnp.tanh(half)


def normed(value, gain, shift):
    center = value - jnp.mean(value, axis=-1, keepdims=True)
    spread = jnp.mean(center * center, axis=-1, keepdims=True)
    return center * lax.rsqrt(spread + EPS) * gain + shift


def mm(a, b):
    return jnp.dot(a, b, preferred_element_type=jnp.float32)


def kernel(
    nodes_hbm, edges_hbm, send_codes, recv_codes, valid_counts, hub_owner,
    ein_hbm, ebias, eout_hbm, egain, eshift, nin_hbm, nbias, nout_hbm, ngain, nshift,
    nodes_out, edges_out,
    hself, hpart, hfar, edges, pre, onehot, scatter, table,
    ein, eout, nin, nout,
    sum_self, sum_part, sum_far,
    hub_own, hub_first, hub_mid, hub_second,
    fub_own, fub_first, fub_mid, fub_second,
    self_send, self_in, far_send, far_in, back_send, back_in, pass_send, pass_in,
    far_send2, far_in2, back_send2, back_in2,
    local_sems, send_sems, recv_sems,
):
    rows = hself.shape[0]
    dim = hself.shape[1]
    count = edges.shape[0]
    tiles = count // TILE
    bf16 = jnp.bfloat16
    me = lax.axis_index("patch")
    region = lax.axis_index("region")
    odd = me % 2
    part = me + 1 - 2 * odd
    onward = (me + 2 - 4 * odd + N_PATCH) % N_PATCH
    source = (me - 2 + 4 * odd + N_PATCH) % N_PATCH
    far = (me - 1 + 2 * odd + N_PATCH) % N_PATCH

    barrier = pltpu.get_barrier_semaphore()
    greeted = [part, onward, source] + [flipped(me, m) for s in HUB_STAGES for m in s if m != 1]
    for other in greeted:
        pl.semaphore_signal(barrier, inc=1, device_id=(region, other), device_id_type=MESH)

    def load(src, dst, index):
        copy = pltpu.make_async_copy(src, dst, local_sems.at[index])
        copy.start()
        return copy

    get_nodes = load(nodes_hbm, hself, 0)
    get_ein0 = load(ein_hbm.at[0], ein.at[0], 1)
    get_edges = load(edges_hbm, edges, 2)
    get_eout = load(eout_hbm, eout, 3)
    get_nin = load(nin_hbm, nin, 4)
    get_nout = load(nout_hbm, nout, 5)
    get_ein1 = load(ein_hbm.at[1], ein.at[1], 6)

    used = [0]

    def send(src, dst, other):
        index = used[0]
        used[0] += 1
        copy = pltpu.make_async_remote_copy(
            src, dst, send_sems.at[index], recv_sems.at[index],
            device_id=(region, other), device_id_type=MESH,
        )
        copy.start()
        return copy

    sent = []

    codes = send_codes[...]
    is_odd = odd == 1
    behind = jnp.where(is_odd, codes + 2 * rows, codes + 4 * rows)
    ahead = jnp.where(is_odd, codes + 2 * rows, codes)
    send_pos = jnp.where(
        codes < rows, behind,
        jnp.where(codes < 2 * rows, codes - rows, jnp.where(codes < 3 * rows, ahead, codes + 3 * rows)),
    )
    rcodes = recv_codes[...]
    behind = jnp.where(is_odd, rcodes + 3 * rows, rcodes + 5 * rows)
    ahead = jnp.where(is_odd, rcodes + 3 * rows, rcodes + rows)
    recv_pos = jnp.where(rcodes < rows, behind, jnp.where(rcodes < 2 * rows, rcodes, ahead))
    behind = jnp.where(is_odd, rcodes + rows, rcodes + 2 * rows)
    ahead = jnp.where(is_odd, rcodes, rcodes - rows)
    add_pos = jnp.where(rcodes < rows, behind, jnp.where(rcodes < 2 * rows, rcodes - rows, ahead))
    block = 128
    lane = lax.broadcasted_iota(jnp.int32, (block, block), 1)
    line = lax.broadcasted_iota(jnp.int32, (3 * rows, block), 0)
    hub_at = 6 * rows
    width = rows // block
    for b in range(count // block):
        send_col = jnp.broadcast_to(send_pos[b : b + 1, :], (block, block)).T
        recv_col = jnp.broadcast_to(recv_pos[b : b + 1, :], (block, block)).T
        for seg in range(7):
            for w in range(width if seg < 6 else 1):
                start = seg * rows + w * block
                col = send_col if seg % 2 == 0 else recv_col
                onehot[b * block : (b + 1) * block, start : start + block] = jnp.where(
                    col == lane + start, 1.0, 0.0
                ).astype(bf16)
        scatter[:, b * block : (b + 1) * block] = jnp.where(
            add_pos[b : b + 1, :] == line, 1.0, 0.0
        ).astype(bf16)
    table[hub_at:, :] = jnp.zeros((block, dim), bf16)

    get_nodes.wait()
    head = hself[0:HUB, :]
    owner0 = hub_owner[0, 0]
    owner1 = hub_owner[1, 0]
    zero_head = jnp.zeros_like(head)
    hub_own[0:HUB, :] = jnp.where(owner0 == me, head, zero_head)
    hub_own[HUB:, :] = jnp.where(owner1 == me, head, zero_head)

    pl.semaphore_wait(barrier, len(greeted))

    def hub_start(src, dst, stage):
        return [send(src, dst.at[j], flipped(me, m)) for j, m in enumerate(HUB_STAGES[stage])]

    def hub_sum(own, got):
        total = own[...].astype(jnp.float32)
        for j in range(3):
            total = total + got[j].astype(jnp.float32)
        return total.astype(bf16)

    step = rows // CHUNKS
    out_part = [
        send(hself.at[pl.ds(i * step, step)], hpart.at[pl.ds(i * step, step)], part)
        for i in range(CHUNKS)
    ]
    hub_a = hub_start(hub_own, hub_first, 0)
    sent += hub_a

    def project(layer, start, h):
        table[start : start + rows, :] = mm(h, ein[layer, 1]).astype(bf16)
        table[start + rows : start + 2 * rows, :] = mm(h, ein[layer, 2]).astype(bf16)

    def project_hub(layer, h):
        table[hub_at : hub_at + HUB, :] = mm(h, ein[layer, 1]).astype(bf16)

    def tile_at(t):
        return pl.ds(pl.multiple_of(t * TILE, TILE), TILE)

    def gather(low, high):
        def body(t, carry):
            at = tile_at(t)
            pre[at, :] += mm(onehot[at, low:high], table[low:high, :])
            return carry

        lax.fori_loop(0, tiles, body, 0)

    def update_edges(layer, low, high):
        valid = valid_counts[0]
        gain = egain[layer : layer + 1, :]
        shift = eshift[layer : layer + 1, :]

        def body(t, carry):
            at = tile_at(t)
            total = pre[at, :] + mm(onehot[at, low:high], table[low:high, :])
            mixed = mm(silu(total).astype(bf16), eout[layer])
            updated = edges[at, :].astype(jnp.float32) + normed(mixed, gain, shift)
            row = lax.broadcasted_iota(jnp.int32, (TILE, 1), 0) + t * TILE
            edges[at, :] = jnp.where(row < valid, updated, 0.0).astype(bf16)
            if layer == LAYERS - 1:
                pltpu.make_async_copy(edges.at[at], edges_out.at[at], local_sems.at[7]).start()
            return carry

        lax.fori_loop(0, tiles, body, 0)

    def update_nodes(layer, h, aggregate):
        total = mm(h, nin[layer, 0]) + mm(aggregate, nin[layer, 1]) + nbias[layer : layer + 1, :]
        mixed = mm(silu(total).astype(bf16), nout[layer])
        gain = ngain[layer : layer + 1, :]
        shift = nshift[layer : layer + 1, :]
        return (h.astype(jnp.float32) + normed(mixed, gain, shift)).astype(bf16)

    def edge_part(layer, own):
        bias = ebias[layer : layer + 1, :]

        def body(t, carry):
            at = tile_at(t)
            total = mm(edges[at, :], ein[layer, 0]) + bias
            if own:
                total = total + mm(onehot[at, 0 : 2 * rows], table[0 : 2 * rows, :])
            pre[at, :] = total
            return carry

        lax.fori_loop(0, tiles, body, 0)

    get_ein0.wait()
    project(0, 0, hself[...])
    get_edges.wait()
    edge_part(0, True)
    out_far = []
    for i in range(CHUNKS):
        out_part[i].wait_recv()
        out_far.append(
            send(hpart.at[pl.ds(i * step, step)], hfar.at[pl.ds(i * step, step)], onward)
        )
        if i == CHUNKS // 2:
            for copy in hub_a:
                copy.wait_recv()
            hub_mid[...] = hub_sum(hub_own, hub_first)
            hub_b = hub_start(hub_mid, hub_second, 1)
    passed = out_far
    sent += hub_b
    project(0, 2 * rows, hpart[...])
    gather(2 * rows, 4 * rows)
    for copy in hub_b:
        copy.wait_recv()
    hub_all = hub_sum(hub_mid, hub_second)
    project_hub(0, hub_all[0:HUB, :])
    for copy in out_far:
        copy.wait_recv()
    project(0, 4 * rows, hfar[...])
    get_eout.wait()
    update_edges(0, 4 * rows, hub_at + block)

    size = rows // PIECES
    values = mm(scatter[0:rows, :], edges[...])
    sum_self[...] = values
    self_send[...] = values.astype(bf16)
    values = mm(scatter[2 * rows : 3 * rows, :], edges[...])
    out_self = [
        send(self_send.at[pl.ds(i * size, size)], self_in.at[pl.ds(i * size, size)], part)
        for i in range(PIECES)
    ]
    sum_far[...] = values
    far_send[...] = values.astype(bf16)
    sum_part[...] = mm(scatter[rows : 2 * rows, :], edges[...])
    out_far = [
        send(far_send.at[pl.ds(i * size, size)], far_in.at[pl.ds(i * size, size)], source)
        for i in range(PIECES)
    ]
    zero_sum = jnp.zeros((HUB, dim), jnp.float32)
    fub_own[...] = (
        jnp.where(owner1 == me, sum_self[0:HUB, :], zero_sum)
        + jnp.where(owner1 == part, sum_part[0:HUB, :], zero_sum)
        + jnp.where(owner1 == far, sum_far[0:HUB, :], zero_sum)
    ).astype(bf16)
    get_ein1.wait()
    edge_part(1, False)
    hub_a = hub_start(fub_own, fub_first, 0)
    sent += out_self + out_far + hub_a
    out_back = []
    out_pass = []
    for i in range(PIECES):
        at = pl.ds(i * size, size)
        mine = sum_part[at, :]
        out_far[i].wait_recv()
        from_far = far_in[at, :].astype(jnp.float32)
        back_send[at, :] = (mine + from_far).astype(bf16)
        out_self[i].wait_recv()
        from_part = self_in[at, :].astype(jnp.float32)
        pass_send[at, :] = (mine + from_part).astype(bf16)
        sum_part[at, :] = mine + from_far + from_part
        out_back.append(send(back_send.at[at], back_in.at[at], part))
        out_pass.append(send(pass_send.at[at], pass_in.at[at], onward))
    for copy in hub_a:
        copy.wait_recv()
    fub_mid[...] = hub_sum(fub_own, fub_first)
    get_nin.wait()
    get_nout.wait()
    for copy in passed:
        copy.wait_send()
    hpart[...] = update_nodes(0, hpart[...], sum_part[...].astype(bf16))
    hub_b = hub_start(fub_mid, fub_second, 1)
    sent += out_back + out_pass + hub_b
    project(1, 2 * rows, hpart[...])
    gather(2 * rows, 4 * rows)
    for copy in out_pass:
        copy.wait_recv()
    hfar_new = update_nodes(
        0, hfar[...], (sum_far[...] + pass_in[...].astype(jnp.float32)).astype(bf16)
    )
    project(1, 4 * rows, hfar_new)
    for copy in hub_b:
        copy.wait_recv()
    hub_new = update_nodes(0, hub_all[HUB:, :], hub_sum(fub_mid, fub_second))
    project_hub(1, hub_new)
    gather(4 * rows, hub_at + block)
    for copy in out_back:
        copy.wait_recv()
    hown = update_nodes(
        0, hself[...], (sum_self[...] + back_in[...].astype(jnp.float32)).astype(bf16)
    )
    project(1, 0, hown)
    update_edges(1, 0, 2 * rows)

    values = mm(scatter[2 * rows : 3 * rows, :], edges[...])
    far_send2[...] = values.astype(bf16)
    sum_part[...] = mm(scatter[rows : 2 * rows, :], edges[...])
    out_far = [
        send(far_send2.at[pl.ds(i * size, size)], far_in2.at[pl.ds(i * size, size)], source)
        for i in range(PIECES)
    ]
    sum_self[...] = mm(scatter[0:rows, :], edges[...])
    out_back = []
    for i in range(PIECES):
        at = pl.ds(i * size, size)
        out_far[i].wait_recv()
        back_send2[at, :] = (sum_part[at, :] + far_in2[at, :].astype(jnp.float32)).astype(bf16)
        out_back.append(send(back_send2.at[at], back_in2.at[at], part))
    sent += out_far + out_back
    for copy in out_back:
        copy.wait_recv()
    for copy in out_part:
        copy.wait_send()
    hself[...] = update_nodes(
        1, hown, (sum_self[...] + back_in2[...].astype(jnp.float32)).astype(bf16)
    )
    put = pltpu.make_async_copy(hself, nodes_out, local_sems.at[8])
    put.start()
    for copy in sent:
        copy.wait_send()
    put.wait()
    pltpu.make_async_copy(edges, edges_out, local_sems.at[7]).wait()


def local(
    nodes, edges, senders, receivers, valid_counts, hub_owner, edge_in, edge_bias, edge_out, edge_gain,
    edge_shift, node_in, node_bias, node_out, node_gain, node_shift,
):
    rows, dim = nodes.shape
    count = edges.shape[0]
    bf16 = jnp.bfloat16
    senders = senders.reshape(count // 128, 128)
    receivers = receivers.reshape(count // 128, 128)
    hbm = pl.BlockSpec(memory_space=pl.ANY)
    vmem = pl.BlockSpec(memory_space=pltpu.VMEM)
    smem = pl.BlockSpec(memory_space=pltpu.SMEM)
    block = pltpu.VMEM((rows, dim), bf16)
    total = pltpu.VMEM((rows, dim), jnp.float32)
    hub = pltpu.VMEM((2 * HUB, dim), bf16)
    hub3 = pltpu.VMEM((3, 2 * HUB, dim), bf16)
    fub = pltpu.VMEM((HUB, dim), bf16)
    fub3 = pltpu.VMEM((3, HUB, dim), bf16)
    places = 6 * rows + 128
    return pl.pallas_call(
        kernel,
        out_shape=(
            jax.ShapeDtypeStruct((rows, dim), bf16),
            jax.ShapeDtypeStruct((count, dim), bf16),
        ),
        in_specs=[hbm, hbm, vmem, vmem, smem, smem, hbm, vmem, hbm, vmem, vmem, hbm, vmem, hbm, vmem, vmem],
        out_specs=(hbm, hbm),
        scratch_shapes=[
            block, block, block,
            pltpu.VMEM((count, dim), bf16),
            pltpu.VMEM((count, dim), jnp.float32),
            pltpu.VMEM((count, places), bf16),
            pltpu.VMEM((3 * rows, count), bf16),
            pltpu.VMEM((places, dim), bf16),
            pltpu.VMEM(edge_in.shape, bf16),
            pltpu.VMEM(edge_out.shape, bf16),
            pltpu.VMEM(node_in.shape, bf16),
            pltpu.VMEM(node_out.shape, bf16),
            total, total, total,
            hub, hub3, hub, hub3,
            fub, fub3, fub, fub3,
            block, block, block, block, block, block, block, block,
            block, block, block, block,
            pltpu.SemaphoreType.DMA((9,)),
            pltpu.SemaphoreType.DMA((64,)),
            pltpu.SemaphoreType.DMA((64,)),
        ],
        compiler_params=pltpu.CompilerParams(
            collective_id=0, has_side_effects=True, vmem_limit_bytes=60 * 1024 * 1024
        ),
        name="steps",
    )(
        nodes, edges, senders, receivers, valid_counts, hub_owner, edge_in, edge_bias, edge_out,
        edge_gain, edge_shift, node_in, node_bias, node_out, node_gain, node_shift,
    )


def solution(mesh):
    split = P(GROUPS, None)
    line = P(GROUPS)
    return jax.shard_map(
        local,
        mesh=mesh,
        in_specs=(split, split, line, line, line, P(None, "region")) + (P(),) * 10,
        out_specs=(split, split),
        check_vma=False,
    )
```

time: 244 us -> 87.9 us (0.36)
  blocking collectives: 82 us -> 0 us
  Pallas kernels: 0 us -> 80.3 us
  local copies, waits for them, and re-layouts: 53.6 us -> 6.01 us
  other arithmetic: 46.7 us -> 0 us
  starting transfers between devices: 25.7 us -> 0 us
  matrix products: 22.4 us -> 0 us
  waiting for transfers between devices: 10.5 us -> 0 us
    psum x4 -> x0, blocking collectives: 82 us -> none  [broadcast_by_axis(): array = lax.psum(array, axis)]
    pallas_call x0 -> x1, Pallas kernels: none -> 80.3 us  [local(): pl.pallas_call(kernel, out_shape=(jax.ShapeDtypeStruct((rows, dim), bf16)...]
    gather x4 -> x0, local copies, waits for them, and re-layouts: 36.8 us -> none  [the longest x2 18.4 us: update_edges(): jnp.take(recv_table, recv_codes, axis=0).astype(jnp.float32)]
    scatter-add x2 -> x0, other arithmetic: 28.9 us -> none  [local(): jax.ops.segment_sum(edges.astype(jnp.float32), receivers, num_segments=3...]
    ppermute x8 -> x0, starting transfers between devices: 25.7 us -> none  [the longest x4 11.4 us: from_behind(): return lax.ppermute(block, axis, route)]
    dot_general x8 -> x0, matrix products: 22.4 us -> none  [the longest x2 14.5 us: update_edges(): jnp.dot(activated, second_weight, preferred_element_type=jnp.float32)]
    ppermute x8 -> x0, waiting for transfers between devices: 10.5 us -> none  [the longest x4 10.5 us: from_behind(): return lax.ppermute(block, axis, route)]
    convert_element_type x4 -> x0, other arithmetic: 7.19 us -> none  [the longest x2 6.11 us: local(): new_edges = jnp.where(is_valid[:, None], updated, 0.0).astype(jnp.bfloat16)]
  transfers between devices with their start and end apart: 8 -> 0, of which waited for: 4 -> 0; matrix products, arithmetic and copies ran while one was open for 3% -> 0% of each run, Pallas kernels for 0% -> 0%
where the time goes in v1:
time: 87.9 us; the launch traced here: 87.6 us
  Pallas kernels  80.3 us (91%)
  local copies, waits for them, and re-layouts  6.01 us (7%)
  between operations  1.29 us (1%)
    pallas_call x1, Pallas kernels, local(): pl.pallas_call(kernel, out_shape=(jax.ShapeDtypeStruct((rows, dim), bf16)...  80.3 us
    unnamed x3, local copies, waits for them, and re-layouts  6.01 us

profile of v1, /device:TPU:4, one launch (start us, length us, event | category | flops | bytes accessed | tf_op | source)
XLA Modules:
  0.0 87.6 jit_solution(17277822204584898032)
XLA Ops:
  1.3 1.3 %copy.18.hub_owner = s32[2,1]{1,0:T(2,128)} copy(s32[2,1]{0,1:T(1,128)} %param.21) | data formatting | bytes 16 | tf_op args[5]
  2.6 80.3 %steps.1 = (bf16[256,512]{1,0:T(8,128)(2,1)}, bf16[2048,512]{1,0:T(8,128)(2,1)}) custom-call(bf16[256,512]{1,0:T(8,128)(2,1)} %nodes_hbm.1, bf16[2048,512]{1,0:T(8,128)(2,1)} %edges_hbm.1, s32[16,128]{1,0:T(8,128)} %bitcast.2, s32[16,128]{1,0:T(8,128)} %bitcast.3, s32[1]{0:T(128)S(6)} %copy.21.valid_counts, s32[2,1]{1,0:T(2,128)} %copy.18.hub_owner, ...), custom_call_target="tpu_custom_call" | custom-call | tf_op jit(solution)/shard_map/steps/pallas_call | solution.py:369
  82.9 1.7 %copy.22 = bf16[256,512]{1,0:T(8,128)(2,1)} copy(bf16[256,512]{1,0:T(8,128)(2,1)} %get-tuple-element.4) | data formatting | bytes 524288
  84.6 3.0 %copy.23 = bf16[2048,512]{1,0:T(8,128)(2,1)} copy(bf16[2048,512]{1,0:T(8,128)(2,1)} %get-tuple-element.5) | data formatting | bytes 4194304

commit v2 on v1

v2 whole, which is shorter than its diff:
```python
import functools

import jax
import jax.numpy as jnp
from jax import lax
from jax.experimental import pallas as pl
from jax.experimental.pallas import tpu as pltpu
from jax.sharding import PartitionSpec as P

HUB = 32
LAYERS = 2
GROUPS = ("region", "patch")
N_PATCH = 16
RUN = N_PATCH // 2
HUB_TURN = 3
FUB_TURN = 2
HUB_AT = 1024
OWN = 1152
PLACES = 1664
MESH = pl.DeviceIdType.MESH
EPS = 1e-05
TILE = 256
CHUNKS = 8
PIECES = 4


def flipped(index, mask):
    for bit in (1, 2, 4, 8):
        if mask & bit:
            index = index + bit - 2 * bit * ((index // bit) % 2)
    return index


class Trip:
    def __init__(self, copy):
        self.copy, self.left, self.landed = copy, False, False

    def wait_send(self):
        if not self.left:
            self.copy.wait_send()
        self.left = True

    def wait_recv(self):
        if not self.landed:
            self.copy.wait_recv()
        self.landed = True


def silu(half):
    return half + half * jnp.tanh(half)


def normed(value, gain, shift):
    share = 1.0 / value.shape[-1]
    center = value - jnp.sum(value, axis=-1, keepdims=True) * share
    spread = jnp.sum(center * center, axis=-1, keepdims=True) * share
    return center * lax.rsqrt(spread + EPS) * gain + shift


def mm(a, b):
    return jnp.dot(a, b, preferred_element_type=jnp.float32)


def kernel(
    nodes_hbm, edges_hbm, send_codes, recv_codes, valid_counts, hub_owner,
    ein_hbm, ebias, eout_hbm, egain, eshift, nin_hbm, nbias, nout_hbm, ngain, nshift,
    nodes_out, edges_out,
    hself, hpart, hfar, edges, pre, onehot, scatter, table,
    ein, eout, nin, nout,
    sum_self, sum_part, sum_far,
    hub_own, hub_got, hub_mid, hub_all, hub_rows,
    aux_own, aux_got, aux_mid, aux_all, aux_rows,
    fub_own, fub_got, fub_mid, fub_all, fub_rows,
    mixed_tile,
    self_send, self_in, far_send, far_in, back_send, back_in, pass_send, pass_in,
    far_send2, far_in2, back_send2, back_in2,
    local_sems, send_sems, recv_sems,
):
    rows = hself.shape[0]
    dim = hself.shape[1]
    count = edges.shape[0]
    tiles = count // TILE
    bf16 = jnp.bfloat16
    me = lax.axis_index("patch")
    region = lax.axis_index("region")
    odd = me % 2
    part = me + 1 - 2 * odd
    onward = (me + 2 - 4 * odd + N_PATCH) % N_PATCH
    source = (me - 2 + 4 * odd + N_PATCH) % N_PATCH
    far = (me - 1 + 2 * odd + N_PATCH) % N_PATCH

    barrier = pltpu.get_barrier_semaphore()
    others = [flipped(me, m) for m in range(1, N_PATCH)]
    greeted = [onward, source] + others
    for other in greeted:
        pl.semaphore_signal(barrier, inc=1, device_id=(region, other), device_id_type=MESH)

    def load(src, dst, index):
        copy = pltpu.make_async_copy(src, dst, local_sems.at[index])
        copy.start()
        return copy

    get_nodes = load(nodes_hbm, hself, 0)
    get_ein0 = load(ein_hbm.at[0], ein.at[0], 1)
    get_edges = load(edges_hbm, edges, 2)
    get_eout = load(eout_hbm, eout, 3)
    get_nin = load(nin_hbm, nin, 4)
    get_nout = load(nout_hbm, nout, 5)
    get_ein1 = load(ein_hbm.at[1], ein.at[1], 6)

    used = [0]

    def send(src, dst, other):
        index = used[0]
        used[0] += 1
        copy = pltpu.make_async_remote_copy(
            src, dst, send_sems.at[index], recv_sems.at[index],
            device_id=(region, other), device_id_type=MESH,
        )
        copy.start()
        trip = Trip(copy)
        sent.append(trip)
        return trip

    sent = []

    codes = send_codes[...]
    is_odd = odd == 1
    behind = jnp.where(is_odd, codes, codes + 2 * rows)
    ahead = jnp.where(is_odd, codes, codes - 2 * rows)
    own = codes - rows + OWN
    send_pos = jnp.where(
        codes < rows, behind,
        jnp.where(codes < 2 * rows, own, jnp.where(codes < 3 * rows, ahead, codes + rows)),
    )
    rcodes = recv_codes[...]
    behind = jnp.where(is_odd, rcodes + rows, rcodes + 3 * rows)
    ahead = jnp.where(is_odd, rcodes + rows, rcodes - rows)
    recv_pos = jnp.where(rcodes < rows, behind, jnp.where(rcodes < 2 * rows, rcodes + OWN, ahead))
    behind = jnp.where(is_odd, rcodes + rows, rcodes + 2 * rows)
    ahead = jnp.where(is_odd, rcodes, rcodes - rows)
    add_pos = jnp.where(rcodes < rows, behind, jnp.where(rcodes < 2 * rows, rcodes - rows, ahead))
    block = 128
    lane = lax.broadcasted_iota(jnp.int32, (block, block), 1)
    line = lax.broadcasted_iota(jnp.int32, (3 * rows, block), 0)
    width = rows // block
    for b in range(count // block):
        send_col = jnp.broadcast_to(send_pos[b : b + 1, :], (block, block)).T
        recv_col = jnp.broadcast_to(recv_pos[b : b + 1, :], (block, block)).T
        starts = (0, rows, 2 * rows, 3 * rows, OWN, OWN + rows, HUB_AT)
        for seg, first in enumerate(starts):
            for w in range(width if seg < 6 else 1):
                start = first + w * block
                col = send_col if seg % 2 == 0 else recv_col
                onehot[b * block : (b + 1) * block, start : start + block] = jnp.where(
                    col == lane + start, 1.0, 0.0
                ).astype(bf16)
        scatter[:, b * block : (b + 1) * block] = jnp.where(
            add_pos[b : b + 1, :] == line, 1.0, 0.0
        ).astype(bf16)
    table[HUB_AT:OWN, :] = jnp.zeros((block, dim), bf16)

    def hub_cut(own, value):
        for piece in range(N_PATCH):
            r, c = divmod(piece, dim // 128)
            own[piece // 2, piece % 2] = value[r * 8 : (r + 1) * 8, c * 128 : (c + 1) * 128]

    get_nodes.wait()
    head = hself[0:HUB, :]
    owner0 = hub_owner[0]
    owner1 = hub_owner[1]
    zero_head = jnp.zeros_like(head)
    hub_cut(hub_own, jnp.where(owner0 == me, head, zero_head))
    hub_cut(aux_own, jnp.where(owner1 == me, head, zero_head))

    pl.semaphore_wait(barrier, len(greeted))

    def hub_scatter(own, got):
        return [send(own.at[other // 2], got.at[m], other) for m, other in enumerate(others)]

    def hub_gather(trips, own, got, mid, everyone):
        total = own[me // 2].astype(jnp.float32)
        for m, trip in enumerate(trips):
            trip.wait_recv()
            total = total + got[m].astype(jnp.float32)
        total = total.astype(bf16)
        mid[0] = total
        everyone[me // 2] = total
        return [send(mid.at[0], everyone.at[me // 2], other) for other in others[1::2]]

    def hub_join(trips, everyone, joined):
        for trip in trips:
            trip.wait_recv()
        for piece in range(N_PATCH):
            r, c = divmod(piece, dim // 128)
            joined[r * 8 : (r + 1) * 8, c * 128 : (c + 1) * 128] = everyone[piece // 2, piece % 2]

    step = rows // CHUNKS
    hub_a = hub_scatter(hub_own, hub_got)
    out_part = [
        send(hself.at[pl.ds(i * step, step)], hpart.at[pl.ds(i * step, step)], part)
        for i in range(CHUNKS)
    ]

    def project(layer, start, h):
        table[start : start + rows, :] = (0.5 * mm(h, ein[layer, 1])).astype(bf16)
        table[start + rows : start + 2 * rows, :] = (0.5 * mm(h, ein[layer, 2])).astype(bf16)

    def project_hub(layer, h):
        table[HUB_AT : HUB_AT + HUB, :] = (0.5 * mm(h, ein[layer, 1])).astype(bf16)

    def tile_at(t):
        return pl.ds(pl.multiple_of(t * TILE, TILE), TILE)

    def gather(low, high):
        def body(t, carry):
            at = tile_at(t)
            pre[at, :] += mm(onehot[at, low:high], table[low:high, :])
            return carry

        lax.fori_loop(0, tiles, body, 0)

    def update_edges(layer, low, high):
        valid = valid_counts[0]
        gain = egain[layer : layer + 1, :]
        shift = eshift[layer : layer + 1, :]

        def collect(t):
            at = tile_at(t)
            pre[at, :] += mm(onehot[at, low:high], table[low:high, :])

        def mix(t):
            mixed_tile[...] = mm(silu(pre[tile_at(t), :]).astype(bf16), eout[layer])

        def finish(t):
            at = tile_at(t)
            updated = edges[at, :].astype(jnp.float32) + normed(mixed_tile[...], gain, shift)
            row = lax.broadcasted_iota(jnp.int32, (TILE, 1), 0) + t * TILE
            edges[at, :] = jnp.where(row < valid, updated, 0.0).astype(bf16)
            if layer == LAYERS - 1:
                pltpu.make_async_copy(edges.at[at], edges_out.at[at], local_sems.at[7]).start()

        def body(t, carry):
            finish(t - 1)
            mix(t)
            collect(t + 1)
            return carry

        collect(0)
        mix(0)
        collect(1)
        lax.fori_loop(1, tiles - 1, body, 0)
        finish(tiles - 2)
        mix(tiles - 1)
        finish(tiles - 1)

    def update_nodes(layer, h, aggregate):
        total = mm(h, nin[layer, 0]) + mm(aggregate, nin[layer, 1]) + nbias[layer : layer + 1, :]
        mixed = mm(silu(0.5 * total).astype(bf16), nout[layer])
        gain = ngain[layer : layer + 1, :]
        shift = nshift[layer : layer + 1, :]
        return (h.astype(jnp.float32) + normed(mixed, gain, shift)).astype(bf16)

    def edge_part(layer, own):
        bias = ebias[layer : layer + 1, :]

        def body(t, carry):
            at = tile_at(t)
            total = 0.5 * (mm(edges[at, :], ein[layer, 0]) + bias)
            if own:
                total = total + mm(onehot[at, OWN:PLACES], table[OWN:PLACES, :])
            pre[at, :] = total
            return carry

        lax.fori_loop(0, tiles, body, 0)

    get_ein0.wait()
    project(0, OWN, hself[...])
    get_edges.wait()
    edge_part(0, True)
    out_far = []
    for i in range(CHUNKS):
        out_part[i].wait_recv()
        out_far.append(
            send(hpart.at[pl.ds(i * step, step)], hfar.at[pl.ds(i * step, step)], onward)
        )
        if i == HUB_TURN:
            hub_b = hub_gather(hub_a, hub_own, hub_got, hub_mid, hub_all)
    passed = out_far
    aux_a = hub_scatter(aux_own, aux_got)
    project(0, 0, hpart[...])
    gather(0, 2 * rows)
    hub_join(hub_b, hub_all, hub_rows)
    project_hub(0, hub_rows[...])
    for copy in out_far:
        copy.wait_recv()
    project(0, 2 * rows, hfar[...])
    get_eout.wait()
    aux_b = hub_gather(aux_a, aux_own, aux_got, aux_mid, aux_all)
    update_edges(0, 2 * rows, OWN)

    size = rows // PIECES
    values = mm(scatter[0:rows, :], edges[...])
    self_send[...] = values.astype(bf16)
    sum_self[...] = values
    values = mm(scatter[2 * rows : 3 * rows, :], edges[...])

    def send_self(i):
        return send(self_send.at[pl.ds(i * size, size)], self_in.at[pl.ds(i * size, size)], part)

    out_self = [send_self(i) for i in range(PIECES // 2)]
    far_send[...] = values.astype(bf16)
    sum_far[...] = values
    sum_part[...] = mm(scatter[rows : 2 * rows, :], edges[...])
    out_far = [
        send(far_send.at[pl.ds(i * size, size)], far_in.at[pl.ds(i * size, size)], source)
        for i in range(PIECES)
    ]
    zero_sum = jnp.zeros((HUB, dim), jnp.float32)
    hub_part = (
        jnp.where(owner1 == me, sum_self[0:HUB, :], zero_sum)
        + jnp.where(owner1 == part, sum_part[0:HUB, :], zero_sum)
        + jnp.where(owner1 == far, sum_far[0:HUB, :], zero_sum)
    ).astype(bf16)
    hub_cut(fub_own, hub_part)
    get_ein1.wait()
    fub_a = hub_scatter(fub_own, fub_got)
    out_self += [send_self(i) for i in range(PIECES // 2, PIECES)]
    edge_part(1, False)
    out_back = []
    out_pass = []
    for i in range(PIECES):
        at = pl.ds(i * size, size)
        mine = sum_part[at, :]
        out_far[i].wait_recv()
        from_far = far_in[at, :].astype(jnp.float32)
        back_send[at, :] = (mine + from_far).astype(bf16)
        sum_part[at, :] = mine + from_far
        out_back.append(send(back_send.at[at], back_in.at[at], part))
        out_self[i].wait_recv()
        from_part = self_in[at, :].astype(jnp.float32)
        pass_send[at, :] = (mine + from_part).astype(bf16)
        sum_part[at, :] = sum_part[at, :] + from_part
        out_pass.append(send(pass_send.at[at], pass_in.at[at], onward))
        if i == FUB_TURN:
            fub_b = hub_gather(fub_a, fub_own, fub_got, fub_mid, fub_all)
    get_nin.wait()
    get_nout.wait()
    for copy in passed:
        copy.wait_send()
    hpart[...] = update_nodes(0, hpart[...], sum_part[...].astype(bf16))
    project(1, 0, hpart[...])
    gather(0, 2 * rows)
    for copy in out_pass:
        copy.wait_recv()
    hfar_new = update_nodes(
        0, hfar[...], (sum_far[...] + pass_in[...].astype(jnp.float32)).astype(bf16)
    )
    project(1, 2 * rows, hfar_new)
    gather(2 * rows, 4 * rows)
    hub_join(aux_b, aux_all, aux_rows)
    hub_join(fub_b, fub_all, fub_rows)
    project_hub(1, update_nodes(0, aux_rows[...], fub_rows[...]))
    for copy in out_back:
        copy.wait_recv()
    hown = update_nodes(
        0, hself[...], (sum_self[...] + back_in[...].astype(jnp.float32)).astype(bf16)
    )
    project(1, OWN, hown)
    update_edges(1, HUB_AT, PLACES)

    values = mm(scatter[2 * rows : 3 * rows, :], edges[...])
    far_send2[...] = values.astype(bf16)
    sum_part[...] = mm(scatter[rows : 2 * rows, :], edges[...])
    out_far = [
        send(far_send2.at[pl.ds(i * size, size)], far_in2.at[pl.ds(i * size, size)], source)
        for i in range(PIECES)
    ]
    sum_self[...] = mm(scatter[0:rows, :], edges[...])
    out_back = []
    for i in range(PIECES):
        at = pl.ds(i * size, size)
        out_far[i].wait_recv()
        back_send2[at, :] = (sum_part[at, :] + far_in2[at, :].astype(jnp.float32)).astype(bf16)
        out_back.append(send(back_send2.at[at], back_in2.at[at], part))
    for copy in out_back:
        copy.wait_recv()
    for copy in out_part:
        copy.wait_send()
    hself[...] = update_nodes(
        1, hown, (sum_self[...] + back_in2[...].astype(jnp.float32)).astype(bf16)
    )
    put = pltpu.make_async_copy(hself, nodes_out, local_sems.at[8])
    put.start()
    for copy in sent:
        copy.wait_send()
    put.wait()
    pltpu.make_async_copy(edges, edges_out, local_sems.at[7]).wait()


def copy_kernel(nodes, edges, nodes_out, edges_out, rows, lines, in_sems, out_sems):
    cut = lines.shape[0] // 4
    spans = [(nodes, nodes_out, rows, pl.ds(0, rows.shape[0]))]
    spans += [(edges, edges_out, lines, pl.ds(i * cut, cut)) for i in range(4)]
    gets = [
        pltpu.make_async_copy(src.at[at], held.at[at], in_sems.at[i])
        for i, (src, _, held, at) in enumerate(spans)
    ]
    puts = [
        pltpu.make_async_copy(held.at[at], dst.at[at], out_sems.at[i])
        for i, (_, dst, held, at) in enumerate(spans)
    ]
    for get in gets:
        get.start()
    for get, put in zip(gets, puts):
        get.wait()
        put.start()
    for put in puts:
        put.wait()


def copied(nodes, edges):
    hbm = pl.BlockSpec(memory_space=pl.ANY)
    return pl.pallas_call(
        copy_kernel,
        out_shape=(
            jax.ShapeDtypeStruct(nodes.shape, nodes.dtype),
            jax.ShapeDtypeStruct(edges.shape, edges.dtype),
        ),
        in_specs=[hbm, hbm],
        out_specs=(hbm, hbm),
        scratch_shapes=[
            pltpu.VMEM(nodes.shape, nodes.dtype),
            pltpu.VMEM(edges.shape, edges.dtype),
            pltpu.SemaphoreType.DMA((5,)),
            pltpu.SemaphoreType.DMA((5,)),
        ],
        compiler_params=pltpu.CompilerParams(vmem_limit_bytes=60 * 1024 * 1024),
        name="place",
    )(nodes, edges)


def local(
    nodes, edges, senders, receivers, valid_counts, hub_owner, edge_in, edge_bias, edge_out, edge_gain,
    edge_shift, node_in, node_bias, node_out, node_gain, node_shift,
):
    rows, dim = nodes.shape
    count = edges.shape[0]
    bf16 = jnp.bfloat16
    hub_owner = hub_owner.reshape(LAYERS)
    senders = senders.reshape(count // 128, 128)
    receivers = receivers.reshape(count // 128, 128)
    hbm = pl.BlockSpec(memory_space=pl.ANY)
    vmem = pl.BlockSpec(memory_space=pltpu.VMEM)
    smem = pl.BlockSpec(memory_space=pltpu.SMEM)
    block = pltpu.VMEM((rows, dim), bf16)
    total = pltpu.VMEM((rows, dim), jnp.float32)

    def hub(pieces):
        return pltpu.VMEM((pieces, 2, 8, 128), bf16)

    hub_set = (hub(RUN), hub(N_PATCH - 1), hub(1), hub(RUN), pltpu.VMEM((HUB, dim), bf16))
    places = PLACES
    out = pl.pallas_call(
        kernel,
        out_shape=(
            jax.ShapeDtypeStruct((rows, dim), bf16),
            jax.ShapeDtypeStruct((count, dim), bf16),
        ),
        in_specs=[hbm, hbm, vmem, vmem, smem, smem, hbm, vmem, hbm, vmem, vmem, hbm, vmem, hbm, vmem, vmem],
        out_specs=(hbm, hbm),
        scratch_shapes=[
            block, block, block,
            pltpu.VMEM((count, dim), bf16),
            pltpu.VMEM((count, dim), jnp.float32),
            pltpu.VMEM((count, places), bf16),
            pltpu.VMEM((3 * rows, count), bf16),
            pltpu.VMEM((places, dim), bf16),
            pltpu.VMEM(edge_in.shape, bf16),
            pltpu.VMEM(edge_out.shape, bf16),
            pltpu.VMEM(node_in.shape, bf16),
            pltpu.VMEM(node_out.shape, bf16),
            total, total, total,
            *hub_set,
            *hub_set,
            *hub_set,
            pltpu.VMEM((TILE, dim), jnp.float32),
            block, block, block, block, block, block, block, block,
            block, block, block, block,
            pltpu.SemaphoreType.DMA((9,)),
            pltpu.SemaphoreType.DMA((112,)),
            pltpu.SemaphoreType.DMA((112,)),
        ],
        compiler_params=pltpu.CompilerParams(
            collective_id=0, has_side_effects=True, vmem_limit_bytes=60 * 1024 * 1024
        ),
        name="steps",
    )(
        nodes, edges, senders, receivers, valid_counts, hub_owner, edge_in, edge_bias, edge_out,
        edge_gain, edge_shift, node_in, node_bias, node_out, node_gain, node_shift,
    )
    return copied(*out)


def solution(mesh):
    split = P(GROUPS, None)
    line = P(GROUPS)
    return jax.shard_map(
        local,
        mesh=mesh,
        in_specs=(split, split, line, line, line, P(None, "region")) + (P(),) * 10,
        out_specs=(split, split),
        check_vma=False,
    )
```

time: 87.9 us -> 76.2 us (0.87)
  local copies, waits for them, and re-layouts: 6.01 us -> 0 us
  Pallas kernels: 80.3 us -> 74.5 us
    pallas_call x1, Pallas kernels: 80.3 us -> 72 us  [local(): pl.pallas_call(kernel, out_shape=(jax.ShapeDtypeStruct((rows, dim), bf16)...]
    unnamed x3 -> x0, local copies, waits for them, and re-layouts: 6.01 us -> none
    pallas_call x0 -> x1, Pallas kernels: none -> 2.52 us  [copied(): pl.pallas_call(copy_kernel, out_shape=(jax.ShapeDtypeStruct(nodes.shape,...]
where the time goes in v2:
time: 76.2 us; the launch traced here: 76 us
  Pallas kernels  74.5 us (98%)
  between operations  1.45 us (2%)
    pallas_call x1, Pallas kernels, local(): pl.pallas_call(kernel, out_shape=(jax.ShapeDtypeStruct((rows, dim), bf16)...  72 us
    pallas_call x1, Pallas kernels, copied(): pl.pallas_call(copy_kernel, out_shape=(jax.ShapeDtypeStruct(nodes.shape,...  2.52 us

profile of v2, /device:TPU:4, one launch (start us, length us, event | category | flops | bytes accessed | tf_op | source)
XLA Modules:
  0.0 76.0 jit_solution(5648845604839366489)
XLA Ops:
  1.3 72.0 %steps.1 = (bf16[256,512]{1,0:T(8,128)(2,1)}, bf16[2048,512]{1,0:T(8,128)(2,1)}) custom-call(bf16[256,512]{1,0:T(8,128)(2,1)} %nodes_hbm.1, bf16[2048,512]{1,0:T(8,128)(2,1)} %edges_hbm.1, s32[16,128]{1,0:T(8,128)} %bitcast.3, s32[16,128]{1,0:T(8,128)} %bitcast.4, s32[1]{0:T(128)S(6)} %copy.18.valid_counts, s32[2]{0:T(128)} %bitcast.5, ...), custom_call_target="tpu_custom_call" | custom-call | tf_op jit(solution)/shard_map/steps/pallas_call | solution.py:464
  73.3 2.5 %place.1 = (bf16[256,512]{1,0:T(8,128)(2,1)}, bf16[2048,512]{1,0:T(8,128)(2,1)}) custom-call(bf16[256,512]{1,0:T(8,128)(2,1)} %get-tuple-element.4.nodes, bf16[2048,512]{1,0:T(8,128)(2,1)} %get-tuple-element.5.edges), custom_call_target="tpu_custom_call" | custom-call | tf_op jit(solution)/shard_map/place/pallas_call | solution.py:424

commit v3 on v2

--- a/solution.py
+++ b/solution.py
@@ -13,7 +13,7 @@
 N_PATCH = 16
 RUN = N_PATCH // 2
 HUB_TURN = 3
-FUB_TURN = 2
+FUB_TURN = 5
 HUB_AT = 1024
 OWN = 1152
 PLACES = 1664
@@ -21,7 +21,7 @@
 EPS = 1e-05
 TILE = 256
 CHUNKS = 8
-PIECES = 4
+PIECES = 8
 
 
 def flipped(index, mask):
@@ -62,8 +62,8 @@
 
 
 def kernel(
-    nodes_hbm, edges_hbm, send_codes, recv_codes, valid_counts, hub_owner,
-    ein_hbm, ebias, eout_hbm, egain, eshift, nin_hbm, nbias, nout_hbm, ngain, nshift,
+    nodes_hbm, edges_hbm, send_hbm, recv_hbm, valid_hbm, owner_hbm,
+    ein_hbm, ebias_hbm, eout_hbm, egain_hbm, eshift_hbm, nin_hbm, nbias_hbm, nout_hbm, ngain_hbm, nshift_hbm,
     nodes_out, edges_out,
     hself, hpart, hfar, edges, pre, onehot, scatter, table,
     ein, eout, nin, nout,
@@ -72,6 +72,7 @@
     aux_own, aux_got, aux_mid, aux_all, aux_rows,
     fub_own, fub_got, fub_mid, fub_all, fub_rows,
     mixed_tile,
+    send_codes, recv_codes, ebias, egain, eshift, nbias, ngain, nshift, valid_counts, hub_owner,
     self_send, self_in, far_send, far_in, back_send, back_in, pass_send, pass_in,
     far_send2, far_in2, back_send2, back_in2,
     local_sems, send_sems, recv_sems,
@@ -101,8 +102,15 @@
         return copy
 
     get_nodes = load(nodes_hbm, hself, 0)
+    get_codes = [load(send_hbm, send_codes, 9), load(recv_hbm, recv_codes, 10)]
+    get_codes += [load(owner_hbm, hub_owner, 11)]
     get_ein0 = load(ein_hbm.at[0], ein.at[0], 1)
     get_edges = load(edges_hbm, edges, 2)
+    vectors = (
+        (ebias_hbm, ebias), (egain_hbm, egain), (eshift_hbm, eshift), (nbias_hbm, nbias),
+        (ngain_hbm, ngain), (nshift_hbm, nshift), (valid_hbm, valid_counts),
+    )
+    get_vectors = [load(src, dst, 12 + i) for i, (src, dst) in enumerate(vectors)]
     get_eout = load(eout_hbm, eout, 3)
     get_nin = load(nin_hbm, nin, 4)
     get_nout = load(nout_hbm, nout, 5)
@@ -124,6 +132,8 @@
 
     sent = []
 
+    for get in get_codes:
+        get.wait()
     codes = send_codes[...]
     is_odd = odd == 1
     behind = jnp.where(is_odd, codes, codes + 2 * rows)
@@ -201,6 +211,7 @@
         send(hself.at[pl.ds(i * step, step)], hpart.at[pl.ds(i * step, step)], part)
         for i in range(CHUNKS)
     ]
+    aux_a = hub_scatter(aux_own, aux_got)
 
     def project(layer, start, h):
         table[start : start + rows, :] = (0.5 * mm(h, ein[layer, 1])).astype(bf16)
@@ -274,6 +285,8 @@
 
         lax.fori_loop(0, tiles, body, 0)
 
+    for get in get_vectors:
+        get.wait()
     get_ein0.wait()
     project(0, OWN, hself[...])
     get_edges.wait()
@@ -287,7 +300,6 @@
         if i == HUB_TURN:
             hub_b = hub_gather(hub_a, hub_own, hub_got, hub_mid, hub_all)
     passed = out_far
-    aux_a = hub_scatter(aux_own, aux_got)
     project(0, 0, hpart[...])
     gather(0, 2 * rows)
     hub_join(hub_b, hub_all, hub_rows)
@@ -296,26 +308,21 @@
         copy.wait_recv()
     project(0, 2 * rows, hfar[...])
     get_eout.wait()
-    aux_b = hub_gather(aux_a, aux_own, aux_got, aux_mid, aux_all)
     update_edges(0, 2 * rows, OWN)
 
     size = rows // PIECES
     values = mm(scatter[0:rows, :], edges[...])
     self_send[...] = values.astype(bf16)
     sum_self[...] = values
-    values = mm(scatter[2 * rows : 3 * rows, :], edges[...])
 
     def send_self(i):
         return send(self_send.at[pl.ds(i * size, size)], self_in.at[pl.ds(i * size, size)], part)
 
     out_self = [send_self(i) for i in range(PIECES // 2)]
+    values = mm(scatter[2 * rows : 3 * rows, :], edges[...])
     far_send[...] = values.astype(bf16)
     sum_far[...] = values
     sum_part[...] = mm(scatter[rows : 2 * rows, :], edges[...])
-    out_far = [
-        send(far_send.at[pl.ds(i * size, size)], far_in.at[pl.ds(i * size, size)], source)
-        for i in range(PIECES)
-    ]
     zero_sum = jnp.zeros((HUB, dim), jnp.float32)
     hub_part = (
         jnp.where(owner1 == me, sum_self[0:HUB, :], zero_sum)
@@ -323,10 +330,15 @@
         + jnp.where(owner1 == far, sum_far[0:HUB, :], zero_sum)
     ).astype(bf16)
     hub_cut(fub_own, hub_part)
+    fub_a = hub_scatter(fub_own, fub_got)
+    out_far = [
+        send(far_send.at[pl.ds(i * size, size)], far_in.at[pl.ds(i * size, size)], source)
+        for i in range(PIECES)
+    ]
+    out_self += [send_self(i) for i in range(PIECES // 2, PIECES)]
     get_ein1.wait()
-    fub_a = hub_scatter(fub_own, fub_got)
-    out_self += [send_self(i) for i in range(PIECES // 2, PIECES)]
     edge_part(1, False)
+    aux_b = hub_gather(aux_a, aux_own, aux_got, aux_mid, aux_all)
     out_back = []
     out_pass = []
     for i in range(PIECES):
@@ -383,19 +395,22 @@
         out_far[i].wait_recv()
         back_send2[at, :] = (sum_part[at, :] + far_in2[at, :].astype(jnp.float32)).astype(bf16)
         out_back.append(send(back_send2.at[at], back_in2.at[at], part))
-    for copy in out_back:
-        copy.wait_recv()
     for copy in out_part:
         copy.wait_send()
-    hself[...] = update_nodes(
-        1, hown, (sum_self[...] + back_in2[...].astype(jnp.float32)).astype(bf16)
-    )
-    put = pltpu.make_async_copy(hself, nodes_out, local_sems.at[8])
-    put.start()
+    pltpu.make_async_copy(edges, edges_out, local_sems.at[7]).wait()
+    puts = []
+    for k in range(2):
+        for copy in out_back[k * PIECES // 2 : (k + 1) * PIECES // 2]:
+            copy.wait_recv()
+        at = pl.ds(k * rows // 2, rows // 2)
+        got = (sum_self[at, :] + back_in2[at, :].astype(jnp.float32)).astype(bf16)
+        hself[at, :] = update_nodes(1, hown[k * rows // 2 : (k + 1) * rows // 2, :], got)
+        puts.append(pltpu.make_async_copy(hself.at[at], nodes_out.at[at], local_sems.at[(8, 0)[k]]))
+        puts[-1].start()
     for copy in sent:
         copy.wait_send()
-    put.wait()
-    pltpu.make_async_copy(edges, edges_out, local_sems.at[7]).wait()
+    for put in puts:
+        put.wait()
 
 
 def copy_kernel(nodes, edges, nodes_out, edges_out, rows, lines, in_sems, out_sems):
@@ -451,8 +466,6 @@
     senders = senders.reshape(count // 128, 128)
     receivers = receivers.reshape(count // 128, 128)
     hbm = pl.BlockSpec(memory_space=pl.ANY)
-    vmem = pl.BlockSpec(memory_space=pltpu.VMEM)
-    smem = pl.BlockSpec(memory_space=pltpu.SMEM)
     block = pltpu.VMEM((rows, dim), bf16)
     total = pltpu.VMEM((rows, dim), jnp.float32)
 
@@ -467,7 +480,7 @@
             jax.ShapeDtypeStruct((rows, dim), bf16),
             jax.ShapeDtypeStruct((count, dim), bf16),
         ),
-        in_specs=[hbm, hbm, vmem, vmem, smem, smem, hbm, vmem, hbm, vmem, vmem, hbm, vmem, hbm, vmem, vmem],
+        in_specs=[hbm] * 16,
         out_specs=(hbm, hbm),
         scratch_shapes=[
             block, block, block,
@@ -485,11 +498,16 @@
             *hub_set,
             *hub_set,
             pltpu.VMEM((TILE, dim), jnp.float32),
+            pltpu.VMEM(senders.shape, jnp.int32),
+            pltpu.VMEM(receivers.shape, jnp.int32),
+            *([pltpu.VMEM(edge_bias.shape, jnp.float32)] * 6),
+            pltpu.SMEM((1,), jnp.int32),
+            pltpu.SMEM((LAYERS,), jnp.int32),
             block, block, block, block, block, block, block, block,
             block, block, block, block,
-            pltpu.SemaphoreType.DMA((9,)),
-            pltpu.SemaphoreType.DMA((112,)),
-            pltpu.SemaphoreType.DMA((112,)),
+            pltpu.SemaphoreType.DMA((19,)),
+            pltpu.SemaphoreType.DMA((144,)),
+            pltpu.SemaphoreType.DMA((144,)),
         ],
         compiler_params=pltpu.CompilerParams(
             collective_id=0, has_side_effects=True, vmem_limit_bytes=60 * 1024 * 1024

time: 76.2 us -> 71.2 us (0.934)
  Pallas kernels: 74.5 us -> 69.6 us
    pallas_call x1, Pallas kernels: 72 us -> 67 us  [local(): pl.pallas_call(kernel, out_shape=(jax.ShapeDtypeStruct((rows, dim), bf16)...]
where the time goes in v3:
time: 71.2 us; the launch traced here: 71 us
  Pallas kernels  69.6 us (98%)
  between operations  1.45 us (2%)
    pallas_call x1, Pallas kernels, local(): pl.pallas_call(kernel, out_shape=(jax.ShapeDtypeStruct((rows, dim), bf16)...  67 us
    pallas_call x1, Pallas kernels, copied(): pl.pallas_call(copy_kernel, out_shape=(jax.ShapeDtypeStruct(nodes.shape,...  2.52 us

profile of v3, /device:TPU:4, one launch (start us, length us, event | category | flops | bytes accessed | tf_op | source)
XLA Modules:
  0.0 71.0 jit_solution(2519880210769401532)
XLA Ops:
  1.3 67.0 %steps.1 = (bf16[256,512]{1,0:T(8,128)(2,1)}, bf16[2048,512]{1,0:T(8,128)(2,1)}) custom-call(bf16[256,512]{1,0:T(8,128)(2,1)} %nodes_hbm.1, bf16[2048,512]{1,0:T(8,128)(2,1)} %edges_hbm.1, s32[16,128]{1,0:T(8,128)} %bitcast.3, s32[16,128]{1,0:T(8,128)} %bitcast.4, s32[1]{0:T(128)S(6)} %copy.18.valid_hbm, s32[2]{0:T(128)} %bitcast.5, ...), custom_call_target="tpu_custom_call" | custom-call | tf_op jit(solution)/shard_map/steps/pallas_call | solution.py:477
  68.3 2.5 %place.1 = (bf16[256,512]{1,0:T(8,128)(2,1)}, bf16[2048,512]{1,0:T(8,128)(2,1)}) custom-call(bf16[256,512]{1,0:T(8,128)(2,1)} %get-tuple-element.4.nodes, bf16[2048,512]{1,0:T(8,128)(2,1)} %get-tuple-element.5.edges), custom_call_target="tpu_custom_call" | custom-call | tf_op jit(solution)/shard_map/place/pallas_call | solution.py:439

commit v4 on v3

--- a/solution.py
+++ b/solution.py
@@ -383,21 +383,22 @@
 
     values = mm(scatter[2 * rows : 3 * rows, :], edges[...])
     far_send2[...] = values.astype(bf16)
-    sum_part[...] = mm(scatter[rows : 2 * rows, :], edges[...])
+    earlier = list(sent)
     out_far = [
         send(far_send2.at[pl.ds(i * size, size)], far_in2.at[pl.ds(i * size, size)], source)
         for i in range(PIECES)
     ]
+    sum_part[...] = mm(scatter[rows : 2 * rows, :], edges[...])
     sum_self[...] = mm(scatter[0:rows, :], edges[...])
+    for copy in earlier:
+        copy.wait_send()
+    pltpu.make_async_copy(edges, edges_out, local_sems.at[7]).wait()
     out_back = []
     for i in range(PIECES):
         at = pl.ds(i * size, size)
         out_far[i].wait_recv()
         back_send2[at, :] = (sum_part[at, :] + far_in2[at, :].astype(jnp.float32)).astype(bf16)
         out_back.append(send(back_send2.at[at], back_in2.at[at], part))
-    for copy in out_part:
-        copy.wait_send()
-    pltpu.make_async_copy(edges, edges_out, local_sems.at[7]).wait()
     puts = []
     for k in range(2):
         for copy in out_back[k * PIECES // 2 : (k + 1) * PIECES // 2]:
@@ -414,9 +415,9 @@
 
 
 def copy_kernel(nodes, edges, nodes_out, edges_out, rows, lines, in_sems, out_sems):
-    cut = lines.shape[0] // 4
+    cut = lines.shape[0] // 8
     spans = [(nodes, nodes_out, rows, pl.ds(0, rows.shape[0]))]
-    spans += [(edges, edges_out, lines, pl.ds(i * cut, cut)) for i in range(4)]
+    spans += [(edges, edges_out, lines, pl.ds(i * cut, cut)) for i in range(8)]
     gets = [
         pltpu.make_async_copy(src.at[at], held.at[at], in_sems.at[i])
         for i, (src, _, held, at) in enumerate(spans)
@@ -447,8 +448,8 @@
         scratch_shapes=[
             pltpu.VMEM(nodes.shape, nodes.dtype),
             pltpu.VMEM(edges.shape, edges.dtype),
-            pltpu.SemaphoreType.DMA((5,)),
-            pltpu.SemaphoreType.DMA((5,)),
+            pltpu.SemaphoreType.DMA((9,)),
+            pltpu.SemaphoreType.DMA((9,)),
         ],
         compiler_params=pltpu.CompilerParams(vmem_limit_bytes=60 * 1024 * 1024),
         name="place",

time: 71.2 us -> 70.7 us (level)
  no operation moved by 1% of the time
where the time goes in v4:
time: 70.7 us; the launch traced here: 70.4 us
  Pallas kernels  69 us (98%)
  between operations  1.45 us (2%)
    pallas_call x1, Pallas kernels, local(): pl.pallas_call(kernel, out_shape=(jax.ShapeDtypeStruct((rows, dim), bf16)...  66.5 us
    pallas_call x1, Pallas kernels, copied(): pl.pallas_call(copy_kernel, out_shape=(jax.ShapeDtypeStruct(nodes.shape,...  2.5 us

profile of v4, /device:TPU:4, one launch (start us, length us, event | category | flops | bytes accessed | tf_op | source)
XLA Modules:
  0.0 70.4 jit_solution(8073155842871917327)
XLA Ops:
  1.3 66.5 %steps.1 = (bf16[256,512]{1,0:T(8,128)(2,1)}, bf16[2048,512]{1,0:T(8,128)(2,1)}) custom-call(bf16[256,512]{1,0:T(8,128)(2,1)} %nodes_hbm.1, bf16[2048,512]{1,0:T(8,128)(2,1)} %edges_hbm.1, s32[16,128]{1,0:T(8,128)} %bitcast.3, s32[16,128]{1,0:T(8,128)} %bitcast.4, s32[1]{0:T(128)S(6)} %copy.18.valid_hbm, s32[2]{0:T(128)} %bitcast.5, ...), custom_call_target="tpu_custom_call" | custom-call | tf_op jit(solution)/shard_map/steps/pallas_call | solution.py:478
  67.8 2.5 %place.1 = (bf16[256,512]{1,0:T(8,128)(2,1)}, bf16[2048,512]{1,0:T(8,128)(2,1)}) custom-call(bf16[256,512]{1,0:T(8,128)(2,1)} %get-tuple-element.4.nodes, bf16[2048,512]{1,0:T(8,128)(2,1)} %get-tuple-element.5.edges), custom_call_target="tpu_custom_call" | custom-call | tf_op jit(solution)/shard_map/place/pallas_call | solution.py:440
